TPU v7x, 256 devices: a whole 4x4x8 slice. The times are simulated.
256 devices in a mesh: fsdp: 16 (over z, core), tp: 16 (over y, x).
Axes of the slice: x: 4, y: 4, z: 8, core: 2. Of those that a mesh axis runs over, the one named last changes fastest.
Arguments:
- w_gate: bfloat16 [4096, 11008], P('fsdp', 'tp'), may hold values from -0.09375 to 0.09375
- low_gate: bfloat16 [4096, 16], P('fsdp'), may hold values from -0.09375 to 0.09375
- high_gate: bfloat16 [16, 11008], P(None, 'tp'), may hold values from -1.5 to 1.5
- w_up: bfloat16 [4096, 11008], P('fsdp', 'tp'), may hold values from -0.09375 to 0.09375
- low_up: bfloat16 [4096, 16], P('fsdp'), may hold values from -0.09375 to 0.09375
- high_up: bfloat16 [16, 11008], P(None, 'tp'), may hold values from -1.5 to 1.5
- w_down: bfloat16 [11008, 4096], P('tp', 'fsdp'), may hold values from -0.0546875 to 0.0546875
- low_down: bfloat16 [11008, 16], P('tp'), may hold values from -0.0546875 to 0.0546875
- high_down: bfloat16 [16, 4096], P(None, 'fsdp'), may hold values from -1.5 to 1.5
- norm_train: float32 [4096], P(('fsdp', 'tp')), may hold values from 0.25 to 1.75
- norm_step: float32 [4096], P(('fsdp', 'tp')), may hold values from -0.3 to 0.3
Outputs:
- serving_gate: bfloat16 [4096, 11008], P(None, 'tp')
- serving_up: bfloat16 [4096, 11008], P(None, 'tp')
- serving_down: bfloat16 [11008, 4096], P('tp')
- serve_norm: bfloat16 [4096], replicated
All inputs are finite; a program needn't handle non-finite values.
Results may differ from a plain program's by a relative error of at most 0.001.
Values may be sent and summed in bfloat16 or wider, within the bound.
A program may use at most 128 MiB of HBM per device.

v0:
```python
import jax
import jax.numpy as jnp
from jax import lax
from jax.sharding import Mesh
from jax.sharding import PartitionSpec as P

FSDP = ("fsdp_0", "fsdp_1")
FSDP_TP = ("fsdp_0", "fsdp_1", "tp_0", "tp_1")
TP = ("tp_0", "tp_1")
mix_rate = 2.0


def gather_turned(arrays, axis, dims):
    turned = [jnp.moveaxis(a, dim, 0) for a, dim in zip(arrays, dims)]
    widths = [t[0].size for t in turned]
    both = jnp.concatenate([t.reshape(-1, w) for t, w in zip(turned, widths)], axis=1)
    whole = lax.all_gather(both, axis, axis=0, tiled=True)
    parts = jnp.split(whole, [sum(widths[:k]) for k in range(1, len(widths))], axis=1)
    return tuple(
        (
            jnp.moveaxis(b.reshape(-1, *t.shape[1:]), 0, dim)
            for b, t, dim in zip(parts, turned, dims)
        )
    )


def laid_out(parts, dim):
    parts = jnp.moveaxis(parts, 0, dim)
    dims = parts.shape
    return parts.reshape(*dims[:dim], dims[dim] * dims[dim + 1], *dims[dim + 2 :])


def all_blocks(x, axes, sequence):
    parts = x[None]
    for k in sequence:
        parts = lax.all_gather(parts, axes[k], axis=0, tiled=True)
    held = [lax.axis_size(axes[k]) for k in reversed(sequence)]
    parts = parts.reshape(*held, *x.shape)
    turned = sorted(range(len(sequence)), key=lambda place: sequence[len(sequence) - 1 - place])
    return parts.transpose(*turned, *range(len(sequence), parts.ndim)).reshape(-1, *x.shape)


def gathered_by_axis(x, axes, sequence, dim):
    return laid_out(all_blocks(x, axes, sequence), dim)


def local(
    w_gate,
    low_gate,
    high_gate,
    w_up,
    low_up,
    high_up,
    w_down,
    low_down,
    high_down,
    norm_train,
    norm_step,
):
    whole_gate = w_gate.astype(jnp.float32) + mix_rate * jnp.dot(
        low_gate, high_gate, preferred_element_type=jnp.float32
    )
    whole_up = w_up.astype(jnp.float32) + mix_rate * jnp.dot(
        low_up, high_up, preferred_element_type=jnp.float32
    )
    whole_down = w_down.astype(jnp.float32) + mix_rate * jnp.dot(
        low_down, high_down, preferred_element_type=jnp.float32
    )
    narrow_gate, narrow_up, narrow_down = (
        whole_gate.astype(jnp.bfloat16),
        whole_up.astype(jnp.bfloat16),
        whole_down.astype(jnp.bfloat16),
    )
    serving_gate, serving_up, serving_down = gather_turned(
        (narrow_gate, narrow_up, narrow_down), FSDP, (0, 0, 1)
    )
    serve_norm = gathered_by_axis(
        (norm_train + norm_step).astype(jnp.bfloat16), FSDP_TP, (0, 2, 3, 1), 0
    )
    return (serving_gate, serving_up, serving_down, serve_norm)


def solution(mesh):
    finer = Mesh(mesh.devices.reshape(8, 2, 4, 4), ("fsdp_0", "fsdp_1", "tp_0", "tp_1"))
    in_specs = (
        P(FSDP, TP),
        P(FSDP, None),
        P(None, TP),
        P(FSDP, TP),
        P(FSDP, None),
        P(None, TP),
        P(TP, FSDP),
        P(TP, None),
        P(None, FSDP),
        P(FSDP_TP),
        P(FSDP_TP),
    )
    out_specs = (P(None, TP), P(None, TP), P(TP, None), P())
    return jax.shard_map(local, mesh=finer, in_specs=in_specs, out_specs=out_specs, check_vma=False)
```

profile of v0, /device:TPU:1, one launch (start us, length us, event | category | flops | bytes accessed | tf_op | source)
XLA Modules:
  0.0 139.7 jit_solution(4759233117201555211)
XLA Ops:
  7.2 0.0 copy-start
  7.2 0.0 all-gather.4.cloned.1.call-start
  7.2 0.7 copy-done
  7.9 1.3 fusion.3
  9.2 1.3 fusion.4
  10.5 0.0 copy-start.3
  10.6 0.0 copy-start.1
  10.6 0.0 copy-start.2
  10.6 1.3 fusion.6
  11.9 1.0 pad_maximum_fusion
  12.9 0.0 all-gather.4.cloned.1.call-update
  13.0 0.0 copy-done.3
  13.0 0.6 dynamic-slice
  14.3 0.2 dynamic-update-slice
  14.5 17.3 %all-reduce = bf16[128]{0:T(256)(128)(2,1)S(1)} all-reduce(bf16[128]{0:T(256)(128)(2,1)S(1)} %dynamic-update-slice), channel_id=2, replica_groups=mesh['fsdp_0'=8,'fsdp_1'=2,'tp_0'=4,'tp_1'=4] {'fsdp_0'}, use_global_device_ids=true, to_apply=%add | all-reduce | flops 128 | bytes 512
  31.8 0.1 reshape.12
  31.9 9.7 %all_gather.17 = bf16[32,16]{1,0:T(8,128)(2,1)S(1)} all-gather(bf16[8,16]{1,0:T(8,128)(2,1)S(1)} %reshape.12), channel_id=1, replica_groups=mesh['fsdp_0'=8,'fsdp_1'=2,'tp_0'=4,'tp_1'=4] {'tp_0'}, dimensions={0}, use_global_device_ids=true | all-gather | bytes 1280 | tf_op jit(solution)/shard_map/all_gather | solution.py:36
  41.6 0.1 copy.16
  41.6 10.1 %all-gather.1 = bf16[4,32,16]{1,2,0:T(8,128)(2,1)S(1)} all-gather(bf16[1,32,16]{1,2,0:T(8,128)(2,1)S(1)} %copy.16), channel_id=1, replica_groups=mesh['fsdp_0'=8,'fsdp_1'=2,'tp_0'=4,'tp_1'=4] {'tp_1'}, dimensions={0}, use_global_device_ids=true | all-gather | bytes 5120 | tf_op jit(solution)/shard_map/all_gather | solution.py:36
  51.8 0.1 copy.17
  51.9 10.0 %all_gather.19 = bf16[256,16]{1,0:T(8,128)(2,1)S(1)} all-gather(bf16[128,16]{1,0:T(8,128)(2,1)S(1)} %bitcast.17), channel_id=1, replica_groups=mesh['fsdp_0'=8,'fsdp_1'=2,'tp_0'=4,'tp_1'=4] {'fsdp_1'}, dimensions={0}, use_global_device_ids=true | all-gather | bytes 12288 | tf_op jit(solution)/shard_map/all_gather | solution.py:36
  61.9 0.7 reshape_reshape.3
  62.6 57.0 %all-gather.4.cloned.1.call-done = bf16[4096,2064]{0,1:T(8,128)(2,1)} async-done(((bf16[256,2064]{0,1:T(8,128)(2,1)}), bf16[4096,2064]{0,1:T(8,128)(2,1)}) %all-gather.4.cloned.1.call-update) | async-done | bytes 16908304 | tf_op jit(solution)/shard_map/all_gather | solution.py:17
  119.6 13.3 %slice_bitcast_fusion = (bf16[688,4096]{1,0:T(8,128)(2,1)}, bf16[4096,688]{0,1:T(8,128)(2,1)}, bf16[4096,688]{0,1:T(8,128)(2,1)}) fusion(bf16[4096,2064]{0,1:T(8,128)(2,1)} %all-gather.4.cloned.1.call-done), kind=kLoop, calls=%fused_computation | loop fusion | bytes 33816576 | tf_op jit(solution)/shard_map/transpose | solution.py:21
  (5 shorter events, 0.0 us)
Async XLA Ops:
  7.2 0.7 copy-start
  7.2 112.4 %all-gather.4.cloned.1.call-start = ((), (), s32[]{:S(2)}) async-start(), calls=%async_computation | async-start | bytes 17965056 | tf_op jit(solution)/shard_map/all_gather | solution.py:17
  10.5 2.4 %copy-start.3 = (u32[256]{0:T(256)S(1)}, u32[256]{0:T(256)}, u32[]{:S(2)}) copy-start(u32[256]{0:T(256)} %constant.7) | copy-start | bytes 3076
  10.6 3.7 %copy-start.1 = (f32[16]{0:T(128)S(1)}, f32[16]{0:T(128)}, u32[]{:S(2)}) copy-start(f32[16]{0:T(128)} %param.20) | copy-start | bytes 196
  10.6 3.7 %copy-start.2 = (f32[16]{0:T(128)S(1)}, f32[16]{0:T(128)}, u32[]{:S(2)}) copy-start(f32[16]{0:T(128)} %param.21) | copy-start | bytes 196
Sparse Core Ops, SparseCore 0:
  13.1 106.4 all-gather.3
where the time goes:
time: 140 us
  waiting for transfers between devices  57 us (41%)
  blocking collectives  47.1 us (34%)
  local copies, waits for them, and re-layouts  15.8 us (11%)
  between operations  14.8 us (11%)
  matrix products  3.94 us (3%)
    all_gather x1, waiting for transfers between devices, gather_turned(): whole = lax.all_gather(both, axis, axis=0, tiled=True)  57 us
    all_gather x3, blocking collectives, all_blocks(): parts = lax.all_gather(parts, axes[k], axis=0, tiled=True)  29.8 us
    unnamed x1, blocking collectives  17.3 us
    transpose x1, local copies, waits for them, and re-layouts, gather_turned(): jnp.moveaxis(b.reshape(-1, *t.shape[1:]), 0, dim)  13.3 us
  transfers between devices with their start and end apart: 1, of which 1 were waited for; matrix products, arithmetic and copies ran while one was open for 1% of the time, Pallas kernels for 0%

commit v1 on v0

--- a/solution.py
+++ b/solution.py
@@ -14,7 +14,10 @@
     turned = [jnp.moveaxis(a, dim, 0) for a, dim in zip(arrays, dims)]
     widths = [t[0].size for t in turned]
     both = jnp.concatenate([t.reshape(-1, w) for t, w in zip(turned, widths)], axis=1)
-    whole = lax.all_gather(both, axis, axis=0, tiled=True)
+    whole = jnp.concatenate(
+        lax.all_to_all(jnp.stack([both] * lax.axis_size(axis)), axis, split_axis=0, concat_axis=0),
+        0,
+    )
     parts = jnp.split(whole, [sum(widths[:k]) for k in range(1, len(widths))], axis=1)
     return tuple(
         (

time: 140 us -> 440 us (3.14)
  blocking collectives: 47.1 us -> 400 us
  waiting for transfers between devices: 57 us -> 0.01 us
  between operations: 14.8 us -> 1.38 us
  starting transfers between devices: 0.04 us -> 10.1 us
  local copies, waits for them, and re-layouts: 15.8 us -> 24 us
    unnamed x1, blocking collectives: 17.3 us -> 372 us
    all_gather x1 -> x0, waiting for transfers between devices: 57 us -> none  [gather_turned(): whole = lax.all_gather(both, axis, axis=0, tiled=True)]
    all_to_all x0 -> x1, starting transfers between devices: none -> 10.1 us  [gather_turned(): lax.all_to_all(jnp.stack([both] * lax.axis_size(axis)), axis, split_axis=...]
    reshape x0 -> x1, local copies, waits for them, and re-layouts: none -> 8.67 us  [gather_turned(): jnp.concatenate(lax.all_to_all(jnp.stack([both] * lax.axis_size(axis)), a...]
    transpose x1, local copies, waits for them, and re-layouts: 13.3 us -> 6.61 us  [gather_turned(): jnp.moveaxis(b.reshape(-1, *t.shape[1:]), 0, dim)]
    another operation x0 -> x1, local copies, waits for them, and re-layouts: none -> 6.16 us  [gather_turned(): jnp.stack([both] * lax.axis_size(axis))]
  transfers between devices with their start and end apart: 1 -> 1, of which waited for: 1 -> 0; matrix products, arithmetic and copies ran while one was open for 1% -> 0% of each run, Pallas kernels for 0% -> 0%
where the time goes in v1:
time: 440 us
  blocking collectives  400 us (91%)
  local copies, waits for them, and re-layouts  24 us (5%)
  starting transfers between devices  10.1 us (2%)
    unnamed x1, blocking collectives  372 us
    all_gather x3, blocking collectives, all_blocks(): parts = lax.all_gather(parts, axes[k], axis=0, tiled=True)  28.5 us
    all_to_all x1, starting transfers between devices, gather_turned(): lax.all_to_all(jnp.stack([both] * lax.axis_size(axis)), axis, split_axis=...  10.1 us
  transfers between devices with their start and end apart: 1, of which 0 were waited for; matrix products, arithmetic and copies ran while one was open for 0% of the time, Pallas kernels for 0%

profile of v1, /device:TPU:1, one launch (start us, length us, event | category | flops | bytes accessed | tf_op | source)
XLA Modules:
  0.0 439.9 jit_solution(18135587386448445910)
XLA Ops:
  0.6 0.0 copy-start
  0.6 0.7 copy-done
  1.4 1.3 fusion.3
  2.7 1.3 fusion.4
  4.0 1.3 fusion.6
  5.3 0.1 pad_maximum_fusion
  5.4 6.2 %stack.2 = bf16[16,256,2064]{1,2,0:T(8,128)(2,1)} broadcast(bf16[256,2064]{0,1:T(8,128)(2,1)S(1)} %pad_maximum_fusion), dimensions={1,2} | broadcast | bytes 17965056 | tf_op jit(solution)/shard_map/stack | solution.py:18
  11.6 10.1 %all-to-all-start = ((bf16[16,256,2064]{1,2,0:T(8,128)(2,1)}), bf16[16,256,2064]{1,2,0:T(8,128)(2,1)}, u32[]{:S(2)}, u32[]{:S(2)}) async-start(bf16[16,256,2064]{1,2,0:T(8,128)(2,1)} %stack.2), calls=%async_computation | async-start | bytes 33816576 | tf_op jit(solution)/shard_map/all_to_all | solution.py:18
  21.7 0.0 copy-done.4
  21.7 0.6 dynamic-slice
  22.9 0.0 copy-done.2
  23.0 0.2 dynamic-update-slice
  23.2 371.9 %all-reduce = bf16[128]{0:T(256)(128)(2,1)S(1)} all-reduce(bf16[128]{0:T(256)(128)(2,1)S(1)} %dynamic-update-slice), channel_id=2, replica_groups=mesh['fsdp_0'=8,'fsdp_1'=2,'tp_0'=4,'tp_1'=4] {'fsdp_0'}, use_global_device_ids=true, to_apply=%add | all-reduce | flops 128 | bytes 512
  395.1 0.1 reshape.18
  395.2 8.7 %all_gather.13 = bf16[32,16]{1,0:T(8,128)(2,1)S(1)} all-gather(bf16[8,16]{1,0:T(8,128)(2,1)S(1)} %reshape.18), channel_id=1, replica_groups=mesh['fsdp_0'=8,'fsdp_1'=2,'tp_0'=4,'tp_1'=4] {'tp_0'}, dimensions={0}, use_global_device_ids=true | all-gather | bytes 1280 | tf_op jit(solution)/shard_map/all_gather | solution.py:39
  403.8 0.1 copy.20
  403.9 9.5 %all-gather.1 = bf16[4,32,16]{1,2,0:T(8,128)(2,1)S(1)} all-gather(bf16[1,32,16]{1,2,0:T(8,128)(2,1)S(1)} %copy.20), channel_id=1, replica_groups=mesh['fsdp_0'=8,'fsdp_1'=2,'tp_0'=4,'tp_1'=4] {'tp_1'}, dimensions={0}, use_global_device_ids=true | all-gather | bytes 5120 | tf_op jit(solution)/shard_map/all_gather | solution.py:39
  413.4 0.1 copy.21
  413.5 10.3 %all_gather.15 = bf16[256,16]{1,0:T(8,128)(2,1)S(1)} all-gather(bf16[128,16]{1,0:T(8,128)(2,1)S(1)} %bitcast.20), channel_id=1, replica_groups=mesh['fsdp_0'=8,'fsdp_1'=2,'tp_0'=4,'tp_1'=4] {'fsdp_1'}, dimensions={0}, use_global_device_ids=true | all-gather | bytes 12288 | tf_op jit(solution)/shard_map/all_gather | solution.py:39
  423.9 0.7 reshape_reshape.3
  424.6 0.0 all-to-all-done
  424.6 8.7 %copy.23 = bf16[16,258,8,256]{3,2,0,1:T(8,128)(2,1)S(1)} copy(bf16[16,258,8,256]{3,2,1,0:T(8,128)(2,1)} %bitcast.8) | data formatting | bytes 33816576 | tf_op jit(solution)/shard_map/reshape | solution.py:17
  433.3 0.0 copy-start.1
  433.3 6.6 %slice_bitcast_fusion = (bf16[688,4096]{1,0:T(8,128)(2,1)}, bf16[4096,688]{0,1:T(8,128)(2,1)}, bf16[4096,688]{0,1:T(8,128)(2,1)}) fusion(bf16[4096,2064]{0,1:T(8,128)(2,1)S(1)} %bitcast.18), kind=kLoop, calls=%fused_computation | loop fusion | bytes 33816576 | tf_op jit(solution)/shard_map/transpose | solution.py:24
  (8 shorter events, 0.1 us)
Async XLA Ops:
  0.6 0.7 copy-start
  11.6 10.1 %copy-start.4 = (u32[256]{0:T(256)S(1)}, u32[256]{0:T(256)}, u32[]{:S(2)}) copy-start(u32[256]{0:T(256)} %constant.7) | copy-start | bytes 3076
  11.6 11.4 %copy-start.2 = (f32[16]{0:T(128)S(1)}, f32[16]{0:T(128)}, u32[]{:S(2)}) copy-start(f32[16]{0:T(128)} %param.20) | copy-start | bytes 196
  11.6 11.4 %copy-start.3 = (f32[16]{0:T(128)S(1)}, f32[16]{0:T(128)}, u32[]{:S(2)}) copy-start(f32[16]{0:T(128)} %param.21) | copy-start | bytes 196
  11.6 413.0 %all-to-all-start = ((bf16[16,256,2064]{1,2,0:T(8,128)(2,1)}), bf16[16,256,2064]{1,2,0:T(8,128)(2,1)}, u32[]{:S(2)}, u32[]{:S(2)}) async-start(bf16[16,256,2064]{1,2,0:T(8,128)(2,1)} %stack.2), calls=%async_computation | async-start | bytes 33816576 | tf_op jit(solution)/shard_map/all_to_all | solution.py:18
  433.3 6.6 %copy-start.1 = (bf16[16,688]{1,0:T(8,128)(2,1)S(1)}, bf16[16,688]{1,0:T(8,128)(2,1)}, u32[]{:S(2)}) copy-start(bf16[16,688]{1,0:T(8,128)(2,1)} %param.13) | copy-start | bytes 66052

commit v2 on v0

--- a/solution.py
+++ b/solution.py
@@ -33,7 +33,16 @@
 def all_blocks(x, axes, sequence):
     parts = x[None]
     for k in sequence:
-        parts = lax.all_gather(parts, axes[k], axis=0, tiled=True)
+
+        def load_figure_now(obj, mesh_name):
+            h_now = lax.axis_size(mesh_name)
+            a_now = lax.all_to_all(
+                jnp.stack([obj] * h_now), axis_name=mesh_name, split_axis=0, concat_axis=0
+            )
+            tile_out = jnp.concatenate(a_now, axis=0)
+            return tile_out
+
+        parts = load_figure_now(parts, axes[k])
     held = [lax.axis_size(axes[k]) for k in reversed(sequence)]
     parts = parts.reshape(*held, *x.shape)
     turned = sorted(range(len(sequence)), key=lambda place: sequence[len(sequence) - 1 - place])

time: 140 us -> 140 us (level)
  waiting for transfers between devices: 57 us -> 65.5 us
  blocking collectives: 47.1 us -> 39.8 us
    all_to_all x0 -> x4, blocking collectives: none -> 39.8 us  [load_figure_now(): lax.all_to_all(jnp.stack([obj] * h_now), axis_name=mesh_name, split_axis=...]
    all_gather x3 -> x0, blocking collectives: 29.8 us -> none  [all_blocks(): parts = lax.all_gather(parts, axes[k], axis=0, tiled=True)]
    unnamed x1 -> x0, blocking collectives: 17.3 us -> none
    all_gather x1, waiting for transfers between devices: 57 us -> 65.5 us  [gather_turned(): whole = lax.all_gather(both, axis, axis=0, tiled=True)]
where the time goes in v2:
time: 140 us
  waiting for transfers between devices  65.5 us (47%)
  blocking collectives  39.8 us (28%)
  local copies, waits for them, and re-layouts  15.2 us (11%)
  between operations  14.1 us (10%)
  matrix products  3.94 us (3%)
    all_gather x1, waiting for transfers between devices, gather_turned(): whole = lax.all_gather(both, axis, axis=0, tiled=True)  65.5 us
    all_to_all x4, blocking collectives, load_figure_now(): lax.all_to_all(jnp.stack([obj] * h_now), axis_name=mesh_name, split_axis=...  39.8 us
    transpose x1, local copies, waits for them, and re-layouts, gather_turned(): jnp.moveaxis(b.reshape(-1, *t.shape[1:]), 0, dim)  13.3 us
  transfers between devices with their start and end apart: 1, of which 1 were waited for; matrix products, arithmetic and copies ran while one was open for 1% of the time, Pallas kernels for 0%

profile of v2, /device:TPU:1, one launch (start us, length us, event | category | flops | bytes accessed | tf_op | source)
XLA Modules:
  0.0 139.7 jit_solution(12873930409085171200)
XLA Ops:
  7.2 0.0 copy-start
  7.2 0.0 all-gather.2.cloned.1.call-start
  7.2 0.7 copy-done
  7.9 1.3 fusion.3
  9.2 1.3 fusion.4
  10.5 0.0 copy-start.1
  10.6 0.0 copy-start.2
  10.6 1.3 fusion.6
  11.9 1.0 pad_maximum_fusion
  12.9 0.0 all-gather.2.cloned.1.call-update
  13.0 0.0 copy-done.1
  13.0 0.0 copy-done.2
  13.0 15.4 %all_to_all.20 = bf16[8,1,16]{2,1,0:T(2,128)(2,1)S(1)} all-to-all(bf16[8,1,16]{2,1,0:T(2,128)(2,1)S(1)} %stack.12), channel_id=1, replica_groups=mesh['fsdp_0'=8,'fsdp_1'=2,'tp_0'=4,'tp_1'=4] {'fsdp_0'}, dimensions={0} | all-to-all | bytes 512 | tf_op jit(solution)/shard_map/all_to_all | solution.py:39
  28.4 8.2 %all_to_all.21 = bf16[4,8,16]{2,1,0:T(8,128)(2,1)S(1)} all-to-all(bf16[4,8,16]{2,1,0:T(8,128)(2,1)S(1)} %stack.13), channel_id=1, replica_groups=mesh['fsdp_0'=8,'fsdp_1'=2,'tp_0'=4,'tp_1'=4] {'tp_0'}, dimensions={0} | all-to-all | bytes 2048 | tf_op jit(solution)/shard_map/all_to_all | solution.py:39
  36.6 0.1 copy.19
  36.7 0.1 reshape.14
  36.8 8.0 %all_to_all.22 = bf16[4,2,256]{2,1,0:T(2,128)(2,1)S(1)} all-to-all(bf16[4,2,256]{2,1,0:T(2,128)(2,1)S(1)} %reshape.14), channel_id=1, replica_groups=mesh['fsdp_0'=8,'fsdp_1'=2,'tp_0'=4,'tp_1'=4] {'tp_1'}, dimensions={0} | all-to-all | bytes 8192 | tf_op jit(solution)/shard_map/all_to_all | solution.py:39
  44.7 0.1 reshape.15
  44.8 0.1 stack_reshape.8
  44.9 8.2 %all_to_all.23 = bf16[2,128,16]{1,2,0:T(8,128)(2,1)S(1)} all-to-all(bf16[2,128,16]{1,2,0:T(8,128)(2,1)S(1)} %pad_maximum_fusion.1), channel_id=1, replica_groups=mesh['fsdp_0'=8,'fsdp_1'=2,'tp_0'=4,'tp_1'=4] {'fsdp_1'}, dimensions={0} | all-to-all | bytes 16384 | tf_op jit(solution)/shard_map/all_to_all | solution.py:39
  53.2 0.1 copy.21
  53.3 0.7 reshape_reshape.7
  54.0 65.5 %all-gather.2.cloned.1.call-done = bf16[4096,2064]{0,1:T(8,128)(2,1)} async-done(((bf16[256,2064]{0,1:T(8,128)(2,1)}), bf16[4096,2064]{0,1:T(8,128)(2,1)}) %all-gather.2.cloned.1.call-update) | async-done | bytes 16908304 | tf_op jit(solution)/shard_map/all_gather | solution.py:17
  119.5 13.3 %slice_bitcast_fusion = (bf16[688,4096]{1,0:T(8,128)(2,1)}, bf16[4096,688]{0,1:T(8,128)(2,1)}, bf16[4096,688]{0,1:T(8,128)(2,1)}) fusion(bf16[4096,2064]{0,1:T(8,128)(2,1)} %all-gather.2.cloned.1.call-done), kind=kLoop, calls=%fused_computation | loop fusion | bytes 33816576 | tf_op jit(solution)/shard_map/transpose | solution.py:21
  (8 shorter events, 0.1 us)
Async XLA Ops:
  7.2 0.7 copy-start
  7.2 112.4 %all-gather.2.cloned.1.call-start = ((), (), s32[]{:S(2)}) async-start(), calls=%async_computation.4 | async-start | bytes 17965056 | tf_op jit(solution)/shard_map/all_gather | solution.py:17
  10.5 2.4 %copy-start.1 = (f32[16]{0:T(128)S(1)}, f32[16]{0:T(128)}, u32[]{:S(2)}) copy-start(f32[16]{0:T(128)} %param.20) | copy-start | bytes 196
  10.6 2.4 %copy-start.2 = (f32[16]{0:T(128)S(1)}, f32[16]{0:T(128)}, u32[]{:S(2)}) copy-start(f32[16]{0:T(128)} %param.21) | copy-start | bytes 196
Sparse Core Ops, SparseCore 0:
  13.1 106.4 all-gather.1
